TPU v7x, 256 devices: a whole 4x4x8 slice. The times are simulated.
256 devices in a mesh: blk: 128 (over z, x, y), fld: 2 (over core).
Axes of the slice: x: 4, y: 4, z: 8, core: 2. Of those that a mesh axis runs over, the one named last changes fastest.
Arguments:
- seed_fine: float32 [8, 1024, 4096], P('fld', 'blk'), may hold values from -6 to 6
- seed_coarse: float32 [8, 256, 4096], P('fld', 'blk'), may hold values from -6 to 6
- saved_fine: float32 [4, 8, 1024, 4096], P(None, 'fld', 'blk'), may hold values from 0.5 to 2
- saved_coarse: float32 [2, 8, 256, 4096], P(None, 'fld', 'blk'), may hold values from 0.5 to 2
- diffusion: float32 [8], P('fld'), may hold values from 0.02 to 0.15
- species_shares: float32 [8], P('fld'), may hold values from 0.1 to 1
- fine_nbr: int32 [1024, 6], P('blk'), may hold values from -1 to 1023, as said below
- coarse_nbr: int32 [256, 6], P('blk'), may hold values from -1 to 255, as said below
- children: int32 [256, 8], P('blk'), may hold values from -1 to 1023, as said below
- fine_counts: int32 [1024], P('blk'), may hold values from 1 to 4
- coarse_counts: int32 [256], P('blk'), may hold values from 1 to 4
Outputs:
- adj_fine: float32 [8, 1024, 4096], P('fld', 'blk')
- adj_coarse: float32 [8, 256, 4096], P('fld', 'blk')
Inputs may be any that keep to these rules, and one draw needn't show every extreme that they name: `fine_nbr`: slot of the block beside each face (first and last along cell dimensions 0, 1, 2), -1 at a wall. The relation is symmetric with faces 2a and 2a+1 paired. Across faces 0 to 3 the neighbour is held by the same index of blk, across face 4 by the same or the one below, across face 5 by the same or the one above. `coarse_nbr`: as for the fine level: symmetric, faces 2a and 2a+1 paired; across faces 0 to 3 the same index of blk, across face 4 the same or the one below, across face 5 the same or the one above. `children`: the fine block that refines each coarse octant, or -1. Every fine block refines exactly one octant. The octants held by index i of blk that are refined are refined by blocks of the indices i + d modulo 128 for d = 0 .. 7, exactly 1 of them by the blocks of each such index.
All inputs are finite; a program needn't handle non-finite values.
Results may differ from a plain program's by a relative error of at most 0.0003.
Values sent between devices are 32-bit elements; how exact they have to be, the bound alone decides.
A program may use at most 128 MiB of HBM per device.

v0:
```python
import functools

import jax
import jax.numpy as jnp
from jax import lax
from jax.experimental import pallas as pl
from jax.experimental.pallas import tpu as pltpu
from jax.sharding import PartitionSpec as P

NSUB = 4
FIELDS = 4
ROWS = 8
LANES = 128
TILES = 32
LINKS = 8
COARSE = FIELDS
HEAT = 0.5
ENERGY = 2.0


def rows_of(x, idx):
    return jnp.take_along_axis(x, idx, axis=0, mode="promise_in_bounds")


def lanes_of(x, idx):
    return jnp.take_along_axis(x, idx, axis=1, mode="promise_in_bounds")


def lane_roll(x, steps):
    steps = steps % LANES
    return x if steps == 0 else pltpu.roll(x, steps, 1)


def row_roll(x, steps):
    return pltpu.roll(x, steps % ROWS, 0)


def kernel(
    n,
    seed_fine, seed_coarse, saved_fine, saved_coarse, diffusion, shares, fine_nbr, coarse_nbr, children,
    fine_counts, coarse_counts,
    out_fine, out_coarse,
    X, FL, FF, GG, PM, MR, W, HS, HR, RS, RR, NI, NL, NR, RT, SH, FM, KM, HN, CN, OC,
    h_send, h_recv, w_send, w_recv, m_send, m_recv, r_send, r_recv,
):
    me = lax.axis_index("blk")
    fld = lax.axis_index("fld")
    partner = {"fld": 1 - fld}

    def at(d):
        return {"blk": lax.rem(me + (d + n), n)}

    barrier = pltpu.get_barrier_semaphore()
    pl.semaphore_signal(barrier, inc=1, device_id=partner, device_id_type=pl.DeviceIdType.MESH)
    for d in range(1, LINKS):
        for way in (d, -d):
            pl.semaphore_signal(barrier, inc=1, device_id=at(way), device_id_type=pl.DeviceIdType.MESH)

    shape = (ROWS, LANES)
    row = lax.broadcasted_iota(jnp.int32, shape, 0)
    lane = lax.broadcasted_iota(jnp.int32, shape, 1)
    kk = lane & 15
    even = (row & 1) == 0
    zero = jnp.zeros(shape, jnp.float32)

    def cols(q):
        return pl.ds(pl.multiple_of(q * LANES, LANES), LANES)

    def spread_rows(values):
        out = jnp.full(shape, values[0])
        for r in range(1, ROWS):
            out = jnp.where(row == r, values[r], out)
        return out

    for f in range(FIELDS):
        RT[f] = jnp.full(shape, diffusion[f])
        SH[f] = jnp.full(shape, shares[f])
        FM[f] = jnp.full(shape, jnp.where((fld == 0) & (f == 0), 1.0, 0.0))
    RT[COARSE] = spread_rows([0.5 * diffusion[r // 2] for r in range(ROWS)])
    SH[COARSE] = spread_rows([shares[r // 2] for r in range(ROWS)])
    FM[COARSE] = jnp.where((row < 2) & (fld == 0), 1.0, 0.0)
    CN[0] = spread_rows([fine_counts[r] for r in range(ROWS)])
    CN[1] = spread_rows([coarse_counts[r % 2] for r in range(ROWS)])
    for level in range(2):
        HN[level] = 1.0 / CN[level].astype(jnp.float32)
        for face in range(6):
            if level == 0:
                raw = spread_rows([fine_nbr[r, face] for r in range(ROWS)])
                base, per, idx = me * 8, 8, raw & 7
            else:
                raw = spread_rows([coarse_nbr[r % 2, face] for r in range(ROWS)])
                base, per, idx = me * 2, 2, (row & 6) + (raw & 1)
            there = raw >= 0
            local = there & (raw >= base) & (raw < base + per)
            NI[level * 6 + face] = idx
            NL[level * 6 + face] = jnp.where(local, 1, 0)
            if face >= 4:
                NR[level * 2 + face - 4] = jnp.where(there & ~local, 1, 0)

    for d in range(LINKS):
        octant, slot = jnp.int32(0), jnp.int32(0)
        for p in range(2):
            for o in range(8):
                child = children[p, o]
                hit = (child >= 0) & ((((child >> 3) - me) & (n - 1)) == d)
                octant = jnp.where(hit, p * 8 + o, octant)
                slot = jnp.where(hit, child & 7, slot)
        OC[d] = octant
        OC[LINKS + d] = slot
    keep = [[jnp.where(children[p, o] < 0, 1.0, 0.0) for o in range(8)] for p in range(2)]
    for ab in range(4):
        halves = [jnp.where(kk < 8, keep[p][2 * ab], keep[p][2 * ab + 1]) for p in range(2)]
        KM[ab] = jnp.where(even, halves[0], halves[1])

    def load_coarse(q, _):
        for f in range(FIELDS):
            X[COARSE, q, 2 * f : 2 * f + 2, :] = seed_coarse[f, :, cols(q)]
        return 0

    lax.fori_loop(0, TILES, load_coarse, 0, unroll=4)

    pl.semaphore_wait(barrier, 2 * (LINKS - 1) + 1)

    def octant_copy(rslot, d):
        return pltpu.make_async_remote_copy(
            src_ref=RS.at[rslot, d], dst_ref=RR.at[rslot, d], send_sem=r_send.at[rslot, d],
            recv_sem=r_recv.at[rslot, d], device_id=at(d), device_id_type=pl.DeviceIdType.MESH,
        )

    def send_octants(rslot):
        for d in (7, 6, 5, 4, 3, 2, 1, 0):
            octant = OC[d]
            p, a, b, c = octant >> 3, (octant >> 2) & 1, (octant >> 1) & 1, octant & 1
            parts = []
            for i in range(8):
                v = X[COARSE, (a * 8 + i) * 2 + b]
                v = jnp.where(jnp.full(shape, c) == 1, lane_roll(v, -8), v)
                v = jnp.where(jnp.full(shape, p) == 1, row_roll(v, -1), v)
                parts.append(v)
            target = RR if d == 0 else RS
            for u in range(2):
                pair = []
                for g in range(2):
                    at_i = u * 4 + g * 2
                    pair.append(jnp.where(kk < 8, parts[at_i], lane_roll(parts[at_i + 1], 8)))
                target[rslot, d, u] = jnp.where(even, pair[0], row_roll(pair[1], 1))
            target[rslot, d, 2] = jnp.full(shape, OC[LINKS + d]).astype(jnp.float32)
            if d:
                octant_copy(rslot, d).start()

    def mask_coarse():
        def one(i, _):
            for b in range(2):
                X[COARSE, i * 2 + b] = X[COARSE, i * 2 + b] * KM[(i >> 3) * 2 + b]
            return 0

        lax.fori_loop(0, 16, one, 0, unroll=4)

    def wait_octants(rslot):
        for d in range(1, LINKS):
            octant_copy(rslot, d).wait_recv()

    spread_idx = [
        [((lane >> 5) + jh * 4) * 16 + h * 8 + ((lane & 15) >> 1) for jh in range(2)] for h in range(2)
    ]

    def add_octants(rslot, f, source):
        mine = [RR[rslot, d, 2] == row.astype(jnp.float32) for d in range(LINKS)]
        for u in range(2):
            for g in range(2):
                total = zero
                for d in range(LINKS):
                    line = jnp.broadcast_to(RR[rslot, d, u, pl.ds(f * 2 + g, 1), :], shape)
                    total = jnp.where(mine[d], line, total)
                total = 0.125 * total
                for h in range(2):
                    i = (u * 4 + g * 2 + h) * 2
                    for jh in range(2):
                        gain = lanes_of(total, spread_idx[h][jh])
                        for q in (i * 2 + jh, (i + 1) * 2 + jh):
                            X[f, q] = source(q) + gain

    def mix_copy(slot):
        return pltpu.make_async_remote_copy(
            src_ref=PM.at[slot], dst_ref=MR.at[slot], send_sem=m_send.at[slot], recv_sem=m_recv.at[slot],
            device_id=partner, device_id_type=pl.DeviceIdType.MESH,
        )

    def part_fine(s):
        def one(q, _):
            total = SH[0] * saved_fine[3 - s, 0, :, cols(q)]
            for f in range(1, FIELDS):
                total = total + SH[f] * saved_fine[3 - s, f, :, cols(q)]
            PM[s, q] = total
            return 0

        lax.fori_loop(0, TILES, one, 0, unroll=4)

    def coarse_rows(c, f, q):
        first = jnp.broadcast_to(saved_coarse[c, f, 0:1, cols(q)], shape)
        return jnp.where(even, first, jnp.broadcast_to(saved_coarse[c, f, 1:2, cols(q)], shape))

    def part_coarse(s):
        def one(q, _):
            total = SH[0] * coarse_rows(1 - s, 0, q)
            for f in range(1, FIELDS):
                total = total + SH[f] * coarse_rows(1 - s, f, q)
            PM[4 + s, q] = total
            return 0

        lax.fori_loop(0, TILES, one, 0, unroll=4)

    def factors(slot, level, temperature):
        mix_copy(slot).wait_recv()

        def one(q, _):
            count = CN[level]
            half = HN[level] * HEAT
            mix = PM[slot, q] + MR[slot, q]
            t = temperature(q)
            saved = []
            for k in range(NSUB):
                inverse = 1.0 / t
                e = half * jnp.exp(-ENERGY * inverse)
                saved.append((inverse, e))
                if k + 1 < NSUB:
                    t = jnp.where(k < count, t + mix * e, t)
            f, g = jnp.ones(shape, jnp.float32), zero
            for k in reversed(range(NSUB)):
                inverse, e = saved[k]
                live = k < count
                g = jnp.where(live, g + e * f, g)
                f = jnp.where(live, f + f * (ENERGY * mix * e * (inverse * inverse)), f)
            FF[slot, q] = f
            GG[slot, q] = g
            return 0

        lax.fori_loop(0, TILES, one, 0, unroll=4)

    def factors_fine(s):
        factors(s, 0, lambda q: saved_fine[3 - s, 0, :, cols(q)])

    def factors_coarse(s):
        factors(4 + s, 1, lambda q: coarse_rows(1 - s, 0, q))

    def w_copy(slot):
        return pltpu.make_async_remote_copy(
            src_ref=W.at[slot], dst_ref=W.at[slot], send_sem=w_send.at[slot], recv_sem=w_recv.at[slot],
            device_id=partner, device_id_type=pl.DeviceIdType.MESH,
        )

    def weights(slot, f, level):
        @pl.when(fld == 0)
        def _():
            source = jnp.where(jnp.full(shape, level) == 1, row & 1, row)

            def one(q, _):
                W[slot, q] = GG[slot, q] * rows_of(X[f, q], source)
                return 0

            lax.fori_loop(0, TILES, one, 0, unroll=8)
            w_copy(slot).start()

        @pl.when(fld == 1)
        def _():
            w_copy(slot).wait_recv()

    def halo_copy(slot, way):
        return pltpu.make_async_remote_copy(
            src_ref=HS.at[slot, way], dst_ref=HR.at[slot, way], send_sem=h_send.at[slot, way],
            recv_sem=h_recv.at[slot, way], device_id=at(1 if way == 0 else -1),
            device_id_type=pl.DeviceIdType.MESH,
        )

    def laplace(v, level, g4, g5, emit):
        idx = [NI[level * 6 + face] for face in range(4)]
        has = [NL[level * 6 + face] > 0 for face in range(4)]

        def ghost(x, face):
            return jnp.where(has[face], rows_of(x, idx[face]), zero)

        for i in range(16):
            pair = [v(2 * i), v(2 * i + 1)]
            up = [lane_roll(x, 16) for x in pair]
            down = [lane_roll(x, -16) for x in pair]
            j_less = [jnp.where(lane < 16, ghost(up[1], 2), up[0]), jnp.where(lane < 16, up[0], up[1])]
            j_more = [
                jnp.where(lane >= 112, down[1], down[0]),
                jnp.where(lane >= 112, ghost(down[0], 3), down[1]),
            ]
            for jh in range(2):
                q = 2 * i + jh
                u, m = q // 16, q % 16
                x = pair[jh]
                i_less = v(q - 2) if i > 0 else ghost(v(30 + jh), 0)
                i_more = v(q + 2) if i < 15 else ghost(v(jh), 1)
                k_less = jnp.where(kk == 0, lane_roll(g4[u], -m), lane_roll(x, 1))
                k_more = jnp.where(kk == 15, lane_roll(g5[u], 15 - m), lane_roll(x, -1))
                total = ((i_less + i_more) + (j_less[jh] + j_more[jh])) + ((k_less + k_more) - 6.0 * x)
                emit(q, x, total)

    def pack(v, k):
        packed = []
        for u in range(2):
            out = zero
            for m in range(16):
                out = jnp.where(kk == m, lane_roll(v(u * 16 + m), m - k), out)
            packed.append(out)
        return packed

    def begin(s, f, level):
        slot = s * 5 + f
        wslot = level * 4 + s
        rate = RT[f]
        share = SH[f]
        scaled = FM[f] > 0

        for q in range(TILES):
            X[f, q] = X[f, q] * jnp.where(scaled, FF[wslot, q], 1.0) + share * W[wslot, q]
        low = pack(lambda q: X[f, q], 0)
        high = pack(lambda q: X[f, q], 15)
        idx4, idx5 = NI[level * 6 + 4], NI[level * 6 + 5]
        has4, has5 = NL[level * 6 + 4] > 0, NL[level * 6 + 5] > 0
        g4 = [jnp.where(has4, rows_of(x, idx4), zero) for x in high]
        g5 = [jnp.where(has5, rows_of(x, idx5), zero) for x in low]

        def emit(q, x, total):
            FL[f, q] = rate * total

        laplace(lambda q: X[f, q], level, g4, g5, emit)
        low_first = pack(lambda q: FL[f, q], 0)
        high_first = pack(lambda q: FL[f, q], 15)
        for u in range(2):
            HS[slot, 0, u] = high[u]
            HS[slot, 0, 2 + u] = high_first[u]
            HS[slot, 1, u] = low[u]
            HS[slot, 1, 2 + u] = low_first[u]
        halo_copy(slot, 0).start()
        halo_copy(slot, 1).start()

    def finish(s, f, level):
        slot = s * 5 + f
        rate = RT[f]
        halo_copy(slot, 0).wait_recv()
        halo_copy(slot, 1).wait_recv()
        idx4, idx5 = NI[level * 6 + 4], NI[level * 6 + 5]
        has4, has5 = NL[level * 6 + 4] > 0, NL[level * 6 + 5] > 0
        far4, far5 = NR[level * 2] > 0, NR[level * 2 + 1] > 0
        r4, r5, g4, g5 = [], [], [], []
        for u in range(2):
            r4.append(jnp.where(far4, rate * rows_of(HR[slot, 0, u], idx4), zero))
            r5.append(jnp.where(far5, rate * rows_of(HR[slot, 1, u], idx5), zero))
        for u in range(2):
            low_first = HS[slot, 1, 2 + u] + r4[u]
            high_first = HS[slot, 0, 2 + u] + r5[u]
            far_low = rows_of(HR[slot, 0, 2 + u], idx4) + rate * HS[slot, 1, u]
            far_high = rows_of(HR[slot, 1, 2 + u], idx5) + rate * HS[slot, 0, u]
            g4.append(jnp.where(has4, rows_of(high_first, idx4), jnp.where(far4, far_low, zero)))
            g5.append(jnp.where(has5, rows_of(low_first, idx5), jnp.where(far5, far_high, zero)))
        for q in range(TILES):
            u, m = q // 16, q % 16
            gain = jnp.where(kk == 15, lane_roll(r5[u], 15 - m), zero)
            FL[f, q] = FL[f, q] + jnp.where(kk == 0, lane_roll(r4[u], -m), gain)
        half_rate = 0.5 * rate

        def emit(q, x, total):
            X[f, q] = X[f, q] + (x + half_rate * total)

        laplace(lambda q: FL[f, q], level, g4, g5, emit)

    send_octants(0)
    part_fine(0)

    @pl.when(fld == 1)
    def _():
        mix_copy(0).start()

    part_coarse(0)

    @pl.when(fld == 1)
    def _():
        mix_copy(4).start()

    mask_coarse()

    @pl.when(fld == 0)
    def _():
        factors_fine(0)
        factors_coarse(0)

    wait_octants(0)
    def take_seed(f, _):
        add_octants(0, f, lambda q: seed_fine[f, :, q * LANES : (q + 1) * LANES])
        return 0

    lax.fori_loop(0, FIELDS, take_seed, 0)
    weights(0, 0, 0)
    weights(4, COARSE, 1)

    def start(f, _):
        begin(0, f, f // 4)
        return 0

    lax.fori_loop(0, FIELDS + 1, start, 0)

    def rest(s, _):
        part_fine(s)

        @pl.when(fld == 1)
        def _():
            mix_copy(s).start()

        return 0

    lax.fori_loop(1, 4, rest, 0)
    part_coarse(1)

    @pl.when(fld == 1)
    def _():
        mix_copy(5).start()

    @pl.when(fld == 0)
    def _():
        factors_fine(1)
        factors_coarse(1)

    def turn(t, _):
        late = jnp.where(t >= 5, 1, 0)
        s = late * (1 + (t - 5) // 4)
        f = jnp.where(t >= 5, lax.rem(t + 3, 4), t)
        level = f // 4
        finish(s, f, level)

        @pl.when(level == 1)
        def _():
            send_octants(1)
            mask_coarse()

        @pl.when((s == 1) & (level == 0))
        def _():
            @pl.when(f == 0)
            def _():
                wait_octants(1)

            add_octants(1, f, lambda q: X[f, q])

        @pl.when((f == 0) | (level == 1))
        def _():
            weights(level * 4 + s + 1, f, level)

        begin(s + 1, f, level)

        @pl.when((f == 3) & (s < 2) & (fld == 0))
        def _():
            factors_fine(s + 2)

        return 0

    lax.fori_loop(0, 13, turn, 0)

    def last(t, _):
        f = lax.rem(t + 4, 5)
        level = f // 4
        finish(3 - 2 * level, f, level)

        @pl.when(level == 0)
        def _():
            for q in range(TILES):
                out_fine[f, :, q * LANES : (q + 1) * LANES] = X[f, q]

        @pl.when(level == 1)
        def _():
            for q in range(TILES):
                for v in range(FIELDS):
                    out_coarse[v, :, q * LANES : (q + 1) * LANES] = X[COARSE, q, 2 * v : 2 * v + 2, :]

        return 0

    lax.fori_loop(0, 5, last, 0)

    for rslot in range(2):
        for d in range(1, LINKS):
            octant_copy(rslot, d).wait_send()
    for s in range(4):
        for f in range(5 if s < 2 else 4):
            for way in range(2):
                halo_copy(s * 5 + f, way).wait_send()

    @pl.when(fld == 0)
    def _():
        for slot in range(6):
            w_copy(slot).wait_send()

    @pl.when(fld == 1)
    def _():
        for slot in range(6):
            mix_copy(slot).wait_send()


def shards(*args):
    n = lax.axis_size("blk")
    seed_fine, seed_coarse = args[0], args[1]
    vmem = pl.BlockSpec(memory_space=pltpu.VMEM)
    smem = pl.BlockSpec(memory_space=pltpu.SMEM)
    tile = (ROWS, LANES)

    def buffer(*lead):
        return pltpu.VMEM((*lead, *tile), jnp.float32)

    def table(*lead):
        return pltpu.VMEM((*lead, *tile), jnp.int32)

    dma = pltpu.SemaphoreType.DMA
    return pl.pallas_call(
        functools.partial(kernel, n),
        out_shape=(
            jax.ShapeDtypeStruct(seed_fine.shape, jnp.float32),
            jax.ShapeDtypeStruct(seed_coarse.shape, jnp.float32),
        ),
        in_specs=[vmem] * 4 + [smem] * 7,
        out_specs=(vmem, vmem),
        scratch_shapes=[
            buffer(5, TILES), buffer(5, TILES),
            buffer(6, TILES), buffer(6, TILES), buffer(6, TILES), buffer(6, TILES), buffer(6, TILES),
            buffer(20, 2, 4), buffer(20, 2, 4),
            buffer(2, LINKS, 3), buffer(2, LINKS, 3),
            table(12), table(12), table(4),
            buffer(5), buffer(5), buffer(5), buffer(4), buffer(2), table(2),
            pltpu.SMEM((2 * LINKS,), jnp.int32),
            dma((20, 2)), dma((20, 2)), dma((6,)), dma((6,)), dma((6,)), dma((6,)), dma((2, LINKS)), dma((2, LINKS)),
        ],
        compiler_params=pltpu.CompilerParams(
            collective_id=0, has_side_effects=True, vmem_limit_bytes=40 * 1024 * 1024
        ),
    )(*args)


def solution(mesh):
    return jax.shard_map(
        shards,
        mesh=mesh,
        in_specs=(
            P("fld", "blk", None),
            P("fld", "blk", None),
            P(None, "fld", "blk", None),
            P(None, "fld", "blk", None),
            P("fld"),
            P("fld"),
            P("blk", None),
            P("blk", None),
            P("blk", None),
            P("blk"),
            P("blk"),
        ),
        out_specs=(P("fld", "blk", None), P("fld", "blk", None)),
        check_vma=False,
    )
```

profile of v0, /device:TPU:1, one launch (start us, length us, event | category | flops | bytes accessed | tf_op | source)
XLA Modules:
  0.0 63.4 jit_solution(2351849969538171225)
XLA Ops:
  0.6 0.0 copy-start
  0.6 1.6 %copy-done = f32[4,4,8,4096]{3,2,1,0:T(8,128)S(1)} copy-done((f32[4,4,8,4096]{3,2,1,0:T(8,128)S(1)}, f32[4,4,8,4096]{3,2,1,0:T(8,128)}, u32[]{:S(2)}) %copy-start) | copy-done | bytes 2097176
  2.2 0.0 copy-start.1
  2.2 1.0 %copy-done.1 = f32[4,8,4096]{2,1,0:T(8,128)S(1)} copy-done((f32[4,8,4096]{2,1,0:T(8,128)S(1)}, f32[4,8,4096]{2,1,0:T(8,128)}, u32[]{:S(2)}) %copy-start.1) | copy-done | bytes 524312
  3.3 0.0 copy-start.2
  3.3 0.9 %copy-done.2 = f32[2,4,2,4096]{3,2,1,0:T(2,128)S(1)} copy-done((f32[2,4,2,4096]{3,2,1,0:T(2,128)S(1)}, f32[2,4,2,4096]{3,2,1,0:T(2,128)}, u32[]{:S(2)}) %copy-start.2) | copy-done | bytes 262168
  4.2 0.0 copy-start.3
  4.2 0.9 %copy-done.3 = f32[4,2,4096]{2,1,0:T(2,128)S(1)} copy-done((f32[4,2,4096]{2,1,0:T(2,128)S(1)}, f32[4,2,4096]{2,1,0:T(2,128)}, u32[]{:S(2)}) %copy-start.3) | copy-done | bytes 131096
  5.1 0.0 copy-start.4
  5.1 0.7 %copy-done.4 = s32[8,6]{1,0:T(8,128)S(1)} copy-done((s32[8,6]{1,0:T(8,128)S(1)}, s32[8,6]{1,0:T(8,128)}, u32[]{:S(2)}) %copy-start.4) | copy-done | bytes 216
  5.8 0.0 copy-start.5
  5.8 0.7 %copy-done.5 = s32[2,6]{1,0:T(2,128)S(1)} copy-done((s32[2,6]{1,0:T(2,128)S(1)}, s32[2,6]{1,0:T(2,128)}, u32[]{:S(2)}) %copy-start.5) | copy-done | bytes 72
  6.5 0.0 copy-start.6
  6.5 0.7 %copy-done.6 = s32[2,8]{1,0:T(2,128)S(1)} copy-done((s32[2,8]{1,0:T(2,128)S(1)}, s32[2,8]{1,0:T(2,128)}, u32[]{:S(2)}) %copy-start.6) | copy-done | bytes 88
  7.2 0.0 copy-start.7
  7.2 0.7 %copy-done.7 = f32[4]{0:T(128)S(1)} copy-done((f32[4]{0:T(128)S(1)}, f32[4]{0:T(128)}, u32[]{:S(2)}) %copy-start.7) | copy-done | bytes 40
  7.8 0.0 copy-start.8
  7.8 0.7 %copy-done.8 = f32[4]{0:T(128)S(1)} copy-done((f32[4]{0:T(128)S(1)}, f32[4]{0:T(128)}, u32[]{:S(2)}) %copy-start.8) | copy-done | bytes 40
  8.5 0.0 copy-start.9
  8.5 0.7 %copy-done.9 = s32[8]{0:T(128)S(1)} copy-done((s32[8]{0:T(128)S(1)}, s32[8]{0:T(128)}, u32[]{:S(2)}) %copy-start.9) | copy-done | bytes 56
  9.1 0.0 copy-start.10
  9.1 0.7 %copy-done.10 = s32[2]{0:T(128)S(1)} copy-done((s32[2]{0:T(128)S(1)}, s32[2]{0:T(128)}, u32[]{:S(2)}) %copy-start.10) | copy-done | bytes 32
  9.8 52.1 %shard_map.122 = (f32[4,8,4096]{2,1,0:T(8,128)S(1)}, f32[4,2,4096]{2,1,0:T(2,128)S(1)}) custom-call(f32[4,8,4096]{2,1,0:T(8,128)S(1)} %copy-done.1, f32[4,2,4096]{2,1,0:T(2,128)S(1)} %copy-done.3, f32[4,4,8,4096]{3,2,1,0:T(8,128)S(1)} %copy-done, f32[2,4,2,4096]{3,2,1,0:T(2,128)S(1)} %copy-done.2, f32[4]{0:T(128)S(1)} %copy-done.7, f32[4]{0:T(128)S(1)} %copy-done.8, ...), custom_call_target="tpu_custom_call" | custom-call | tf_op jit(solution)/shard_map/pallas_call | solution.py:514
  61.9 0.8 %copy.15 = f32[4,8,4096]{2,1,0:T(8,128)} copy(f32[4,8,4096]{2,1,0:T(8,128)S(1)} %get-tuple-element.4) | data formatting | bytes 1048576
  62.7 0.7 %copy.16 = f32[4,2,4096]{2,1,0:T(2,128)} copy(f32[4,2,4096]{2,1,0:T(2,128)S(1)} %get-tuple-element.5) | data formatting | bytes 262144
Async XLA Ops:
  0.6 1.6 %copy-start = (f32[4,4,8,4096]{3,2,1,0:T(8,128)S(1)}, f32[4,4,8,4096]{3,2,1,0:T(8,128)}, u32[]{:S(2)}) copy-start(f32[4,4,8,4096]{3,2,1,0:T(8,128)} %saved_fine.1) | copy-start | bytes 6291460
  2.2 1.0 %copy-start.1 = (f32[4,8,4096]{2,1,0:T(8,128)S(1)}, f32[4,8,4096]{2,1,0:T(8,128)}, u32[]{:S(2)}) copy-start(f32[4,8,4096]{2,1,0:T(8,128)} %seed_fine.1) | copy-start | bytes 1572868
  3.3 0.9 %copy-start.2 = (f32[2,4,2,4096]{3,2,1,0:T(2,128)S(1)}, f32[2,4,2,4096]{3,2,1,0:T(2,128)}, u32[]{:S(2)}) copy-start(f32[2,4,2,4096]{3,2,1,0:T(2,128)} %saved_coarse.1) | copy-start | bytes 786436
  4.2 0.9 %copy-start.3 = (f32[4,2,4096]{2,1,0:T(2,128)S(1)}, f32[4,2,4096]{2,1,0:T(2,128)}, u32[]{:S(2)}) copy-start(f32[4,2,4096]{2,1,0:T(2,128)} %seed_coarse.1) | copy-start | bytes 393220
  5.1 0.7 %copy-start.4 = (s32[8,6]{1,0:T(8,128)S(1)}, s32[8,6]{1,0:T(8,128)}, u32[]{:S(2)}) copy-start(s32[8,6]{1,0:T(8,128)} %fine_nbr.1) | copy-start | bytes 580
  5.8 0.7 %copy-start.5 = (s32[2,6]{1,0:T(2,128)S(1)}, s32[2,6]{1,0:T(2,128)}, u32[]{:S(2)}) copy-start(s32[2,6]{1,0:T(2,128)} %coarse_nbr.1) | copy-start | bytes 148
  6.5 0.7 %copy-start.6 = (s32[2,8]{1,0:T(2,128)S(1)}, s32[2,8]{1,0:T(2,128)}, u32[]{:S(2)}) copy-start(s32[2,8]{1,0:T(2,128)} %children.1) | copy-start | bytes 196
  7.2 0.7 %copy-start.7 = (f32[4]{0:T(128)S(1)}, f32[4]{0:T(128)}, u32[]{:S(2)}) copy-start(f32[4]{0:T(128)} %diffusion.1) | copy-start | bytes 52
  7.8 0.7 %copy-start.8 = (f32[4]{0:T(128)S(1)}, f32[4]{0:T(128)}, u32[]{:S(2)}) copy-start(f32[4]{0:T(128)} %shares.1) | copy-start | bytes 52
  8.5 0.7 %copy-start.9 = (s32[8]{0:T(128)S(1)}, s32[8]{0:T(128)}, u32[]{:S(2)}) copy-start(s32[8]{0:T(128)} %fine_counts.1) | copy-start | bytes 100
  9.1 0.7 %copy-start.10 = (s32[2]{0:T(128)S(1)}, s32[2]{0:T(128)}, u32[]{:S(2)}) copy-start(s32[2]{0:T(128)} %coarse_counts.1) | copy-start | bytes 28
where the time goes:
time: 63.7 us; the launch traced here: 63.4 us
  Pallas kernels  52.1 us (82%)
  local copies, waits for them, and re-layouts  10.6 us (17%)
  between operations  0.66 us (1%)
    pallas_call x1, Pallas kernels, shards(): pl.pallas_call(functools.partial(kernel, n), out_shape=(jax.ShapeDtypeStr...  52.1 us
    unnamed x24, local copies, waits for them, and re-layouts  10.6 us

commit v1 on v0

--- a/solution.py
+++ b/solution.py
@@ -37,9 +37,11 @@
 
 def kernel(
     n,
+    seed_fine_in, seed_coarse_in, saved_fine_in, saved_coarse_in, diffusion_in, shares_in, fine_nbr_in, coarse_nbr_in,
+    children_in, fine_counts_in, coarse_counts_in,
+    out_fine, out_coarse,
     seed_fine, seed_coarse, saved_fine, saved_coarse, diffusion, shares, fine_nbr, coarse_nbr, children,
-    fine_counts, coarse_counts,
-    out_fine, out_coarse,
+    fine_counts, coarse_counts, in_sem,
     X, FL, FF, GG, PM, MR, W, HS, HR, RS, RR, NI, NL, NR, RT, SH, FM, KM, HN, CN, OC,
     h_send, h_recv, w_send, w_recv, m_send, m_recv, r_send, r_recv,
 ):
@@ -56,6 +58,20 @@
         for way in (d, -d):
             pl.semaphore_signal(barrier, inc=1, device_id=at(way), device_id_type=pl.DeviceIdType.MESH)
 
+    small = [
+        pltpu.make_async_copy(source, target, in_sem.at[i])
+        for i, (source, target) in enumerate((
+            (children_in, children), (seed_coarse_in, seed_coarse), (diffusion_in, diffusion), (shares_in, shares),
+            (fine_nbr_in, fine_nbr), (coarse_nbr_in, coarse_nbr), (fine_counts_in, fine_counts),
+            (coarse_counts_in, coarse_counts), (saved_coarse_in, saved_coarse), (seed_fine_in, seed_fine),
+        ))
+    ]
+    large = [
+        pltpu.make_async_copy(saved_fine_in.at[3 - s], saved_fine.at[3 - s], in_sem.at[10 + s]) for s in range(4)
+    ]
+    for copy in (*small[:8], large[0], *small[8:], *large[1:]):
+        copy.start()
+
     shape = (ROWS, LANES)
     row = lax.broadcasted_iota(jnp.int32, shape, 0)
     lane = lax.broadcasted_iota(jnp.int32, shape, 1)
@@ -65,6 +81,9 @@
 
     def cols(q):
         return pl.ds(pl.multiple_of(q * LANES, LANES), LANES)
+
+    for copy in small[:8]:
+        copy.wait()
 
     def spread_rows(values):
         out = jnp.full(shape, values[0])
@@ -369,26 +388,48 @@
         laplace(lambda q: FL[f, q], level, g4, g5, emit)
 
     send_octants(0)
-    part_fine(0)
-
-    @pl.when(fld == 1)
-    def _():
-        mix_copy(0).start()
-
-    part_coarse(0)
-
-    @pl.when(fld == 1)
-    def _():
-        mix_copy(4).start()
-
+    for copy in (*large, small[8]):
+        copy.wait()
+
+    def parts(s, _):
+        part_fine(s)
+
+        @pl.when(fld == 1)
+        def _():
+            mix_copy(s).start()
+
+        return 0
+
+    lax.fori_loop(0, 4, parts, 0)
+
+    def parts_coarse(s, _):
+        part_coarse(s)
+
+        @pl.when(fld == 1)
+        def _():
+            mix_copy(4 + s).start()
+
+        return 0
+
+    lax.fori_loop(0, 2, parts_coarse, 0)
     mask_coarse()
 
     @pl.when(fld == 0)
     def _():
-        factors_fine(0)
-        factors_coarse(0)
-
+        def fine(s, _):
+            factors_fine(s)
+            return 0
+
+        def coarse(s, _):
+            factors_coarse(s)
+            return 0
+
+        lax.fori_loop(0, 4, fine, 0)
+        lax.fori_loop(0, 2, coarse, 0)
+
+    small[9].wait()
     wait_octants(0)
+
     def take_seed(f, _):
         add_octants(0, f, lambda q: seed_fine[f, :, q * LANES : (q + 1) * LANES])
         return 0
@@ -402,27 +443,6 @@
         return 0
 
     lax.fori_loop(0, FIELDS + 1, start, 0)
-
-    def rest(s, _):
-        part_fine(s)
-
-        @pl.when(fld == 1)
-        def _():
-            mix_copy(s).start()
-
-        return 0
-
-    lax.fori_loop(1, 4, rest, 0)
-    part_coarse(1)
-
-    @pl.when(fld == 1)
-    def _():
-        mix_copy(5).start()
-
-    @pl.when(fld == 0)
-    def _():
-        factors_fine(1)
-        factors_coarse(1)
 
     def turn(t, _):
         late = jnp.where(t >= 5, 1, 0)
@@ -449,10 +469,6 @@
             weights(level * 4 + s + 1, f, level)
 
         begin(s + 1, f, level)
-
-        @pl.when((f == 3) & (s < 2) & (fld == 0))
-        def _():
-            factors_fine(s + 2)
 
         return 0
 
@@ -501,7 +517,7 @@
     n = lax.axis_size("blk")
     seed_fine, seed_coarse = args[0], args[1]
     vmem = pl.BlockSpec(memory_space=pltpu.VMEM)
-    smem = pl.BlockSpec(memory_space=pltpu.SMEM)
+    hbm = pl.BlockSpec(memory_space=pltpu.HBM)
     tile = (ROWS, LANES)
 
     def buffer(*lead):
@@ -514,12 +530,15 @@
     return pl.pallas_call(
         functools.partial(kernel, n),
         out_shape=(
-            jax.ShapeDtypeStruct(seed_fine.shape, jnp.float32),
-            jax.ShapeDtypeStruct(seed_coarse.shape, jnp.float32),
+            pltpu.VMEM(seed_fine.shape, jnp.float32),
+            pltpu.VMEM(seed_coarse.shape, jnp.float32),
         ),
-        in_specs=[vmem] * 4 + [smem] * 7,
+        in_specs=[hbm] * 11,
         out_specs=(vmem, vmem),
         scratch_shapes=[
+            *(pltpu.VMEM(x.shape, jnp.float32) for x in args[:4]),
+            *(pltpu.SMEM(x.shape, x.dtype) for x in args[4:]),
+            dma((14,)),
             buffer(5, TILES), buffer(5, TILES),
             buffer(6, TILES), buffer(6, TILES), buffer(6, TILES), buffer(6, TILES), buffer(6, TILES),
             buffer(20, 2, 4), buffer(20, 2, 4),
@@ -530,7 +549,7 @@
             dma((20, 2)), dma((20, 2)), dma((6,)), dma((6,)), dma((6,)), dma((6,)), dma((2, LINKS)), dma((2, LINKS)),
         ],
         compiler_params=pltpu.CompilerParams(
-            collective_id=0, has_side_effects=True, vmem_limit_bytes=40 * 1024 * 1024
+            collective_id=0, has_side_effects=True, vmem_limit_bytes=62_000_000
         ),
     )(*args)
 

time: 63.7 us -> 54.8 us (0.86)
  local copies, waits for them, and re-layouts: 10.6 us -> 1.45 us
    unnamed x24 -> x2, local copies, waits for them, and re-layouts: 10.6 us -> 1.45 us
where the time goes in v1:
time: 54.8 us; the launch traced here: 54.7 us
  Pallas kernels  52.6 us (96%)
  local copies, waits for them, and re-layouts  1.45 us (3%)
  between operations  0.64 us (1%)
    pallas_call x1, Pallas kernels, shards(): pl.pallas_call(functools.partial(kernel, n), out_shape=(pltpu.VMEM(seed_f...  52.6 us
    unnamed x2, local copies, waits for them, and re-layouts  1.45 us

profile of v1, /device:TPU:1, one launch (start us, length us, event | category | flops | bytes accessed | tf_op | source)
XLA Modules:
  0.0 54.7 jit_solution(11362868838967967736)
XLA Ops:
  0.6 52.6 %shard_map.122 = (f32[4,8,4096]{2,1,0:T(8,128)S(1)}, f32[4,2,4096]{2,1,0:T(2,128)S(1)}) custom-call(f32[4,8,4096]{2,1,0:T(8,128)} %seed_fine_in.1, f32[4,2,4096]{2,1,0:T(2,128)} %seed_coarse_in.1, f32[4,4,8,4096]{3,2,1,0:T(8,128)} %saved_fine_in.1, f32[2,4,2,4096]{3,2,1,0:T(2,128)} %saved_coarse_in.1, f32[4]{0:T(128)} %diffusion_in.1, f32[4]{0:T(128)} %shares_in.1, ...), custom_call_target="tpu_custom_call" | custom-call | tf_op jit(solution)/shard_map/pallas_call | solution.py:530
  53.2 0.8 %copy.15 = f32[4,8,4096]{2,1,0:T(8,128)} copy(f32[4,8,4096]{2,1,0:T(8,128)S(1)} %get-tuple-element.2) | data formatting | bytes 1048576
  54.0 0.7 %copy.16 = f32[4,2,4096]{2,1,0:T(2,128)} copy(f32[4,2,4096]{2,1,0:T(2,128)S(1)} %get-tuple-element.3) | data formatting | bytes 262144

commit v2 on v1

--- a/solution.py
+++ b/solution.py
@@ -42,7 +42,7 @@
     out_fine, out_coarse,
     seed_fine, seed_coarse, saved_fine, saved_coarse, diffusion, shares, fine_nbr, coarse_nbr, children,
     fine_counts, coarse_counts, in_sem,
-    X, FL, FF, GG, PM, MR, W, HS, HR, RS, RR, NI, NL, NR, RT, SH, FM, KM, HN, CN, OC,
+    MX, X, FL, FF, GG, PM, MR, W, HS, HR, RS, RR, NI, NL, NR, RT, SH, FM, KM, HN, CN, OC,
     h_send, h_recv, w_send, w_recv, m_send, m_recv, r_send, r_recv,
 ):
     me = lax.axis_index("blk")
@@ -291,6 +291,18 @@
             device_id_type=pl.DeviceIdType.MESH,
         )
 
+    def stencil_matrix():
+        def one(r, _):
+            source = r * ROWS * 2 + lax.broadcasted_iota(jnp.int32, (2 * ROWS, 2 * LANES), 0)
+            target = lax.broadcasted_iota(jnp.int32, (2 * ROWS, 2 * LANES), 1)
+            apart = jnp.abs(source - target)
+            near = (apart == 16) | ((apart == 1) & ((source >> 4) == (target >> 4)))
+            entry = jnp.where(near, 1.0, jnp.where(apart == 0, -6.0, 0.0))
+            MX[pl.ds(pl.multiple_of(r * ROWS * 2, ROWS * 2), ROWS * 2), :] = entry.astype(jnp.bfloat16)
+            return 0
+
+        lax.fori_loop(0, 16, one, 0)
+
     def laplace(v, level, g4, g5, emit):
         idx = [NI[level * 6 + face] for face in range(4)]
         has = [NL[level * 6 + face] > 0 for face in range(4)]
@@ -298,25 +310,32 @@
         def ghost(x, face):
             return jnp.where(has[face], rows_of(x, idx[face]), zero)
 
+        matrix = MX[...]
+        planes = jnp.concatenate(
+            [jnp.concatenate([v(2 * i + jh) for i in range(16)], axis=0) for jh in range(2)], axis=1
+        )
+        inner = None
+        for piece in range(3):
+            rounded = planes.astype(jnp.bfloat16)
+            term = jnp.dot(rounded, matrix, preferred_element_type=jnp.float32)
+            inner = term if inner is None else inner + term
+            if piece < 2:
+                planes = planes - rounded.astype(jnp.float32)
+
         for i in range(16):
-            pair = [v(2 * i), v(2 * i + 1)]
-            up = [lane_roll(x, 16) for x in pair]
-            down = [lane_roll(x, -16) for x in pair]
-            j_less = [jnp.where(lane < 16, ghost(up[1], 2), up[0]), jnp.where(lane < 16, up[0], up[1])]
-            j_more = [
-                jnp.where(lane >= 112, down[1], down[0]),
-                jnp.where(lane >= 112, ghost(down[0], 3), down[1]),
+            j_edge = [
+                jnp.where(lane < 16, ghost(lane_roll(v(2 * i + 1), 16), 2), zero),
+                jnp.where(lane >= 112, ghost(lane_roll(v(2 * i), -16), 3), zero),
             ]
             for jh in range(2):
                 q = 2 * i + jh
                 u, m = q // 16, q % 16
-                x = pair[jh]
                 i_less = v(q - 2) if i > 0 else ghost(v(30 + jh), 0)
                 i_more = v(q + 2) if i < 15 else ghost(v(jh), 1)
-                k_less = jnp.where(kk == 0, lane_roll(g4[u], -m), lane_roll(x, 1))
-                k_more = jnp.where(kk == 15, lane_roll(g5[u], 15 - m), lane_roll(x, -1))
-                total = ((i_less + i_more) + (j_less[jh] + j_more[jh])) + ((k_less + k_more) - 6.0 * x)
-                emit(q, x, total)
+                k_edge = jnp.where(kk == 15, lane_roll(g5[u], 15 - m), zero)
+                k_edge = jnp.where(kk == 0, lane_roll(g4[u], -m), k_edge)
+                plane = inner[i * ROWS : (i + 1) * ROWS, jh * LANES : (jh + 1) * LANES]
+                emit(q, v(q), ((i_less + i_more) + (j_edge[jh] + k_edge)) + plane)
 
     def pack(v, k):
         packed = []
@@ -388,6 +407,7 @@
         laplace(lambda q: FL[f, q], level, g4, g5, emit)
 
     send_octants(0)
+    stencil_matrix()
     for copy in (*large, small[8]):
         copy.wait()
 
@@ -539,6 +559,7 @@
             *(pltpu.VMEM(x.shape, jnp.float32) for x in args[:4]),
             *(pltpu.SMEM(x.shape, x.dtype) for x in args[4:]),
             dma((14,)),
+            pltpu.VMEM((2 * LANES, 2 * LANES), jnp.bfloat16),
             buffer(5, TILES), buffer(5, TILES),
             buffer(6, TILES), buffer(6, TILES), buffer(6, TILES), buffer(6, TILES), buffer(6, TILES),
             buffer(20, 2, 4), buffer(20, 2, 4),

time: 54.8 us -> 54 us (0.985)
  Pallas kernels: 52.6 us -> 51.8 us
    pallas_call x1, Pallas kernels: 52.6 us -> 51.8 us  [shards(): pl.pallas_call(functools.partial(kernel, n), out_shape=(pltpu.VMEM(seed_f...]
where the time goes in v2:
time: 54 us; the launch traced here: 53.9 us
  Pallas kernels  51.8 us (96%)
  local copies, waits for them, and re-layouts  1.45 us (3%)
  between operations  0.64 us (1%)
    pallas_call x1, Pallas kernels, shards(): pl.pallas_call(functools.partial(kernel, n), out_shape=(pltpu.VMEM(seed_f...  51.8 us
    unnamed x2, local copies, waits for them, and re-layouts  1.45 us

profile of v2, /device:TPU:1, one launch (start us, length us, event | category | flops | bytes accessed | tf_op | source)
XLA Modules:
  0.0 53.9 jit_solution(16425349858576821336)
XLA Ops:
  0.6 51.8 %shard_map.122 = (f32[4,8,4096]{2,1,0:T(8,128)S(1)}, f32[4,2,4096]{2,1,0:T(2,128)S(1)}) custom-call(f32[4,8,4096]{2,1,0:T(8,128)} %seed_fine_in.1, f32[4,2,4096]{2,1,0:T(2,128)} %seed_coarse_in.1, f32[4,4,8,4096]{3,2,1,0:T(8,128)} %saved_fine_in.1, f32[2,4,2,4096]{3,2,1,0:T(2,128)} %saved_coarse_in.1, f32[4]{0:T(128)} %diffusion_in.1, f32[4]{0:T(128)} %shares_in.1, ...), custom_call_target="tpu_custom_call" | custom-call | tf_op jit(solution)/shard_map/pallas_call | solution.py:550
  52.4 0.8 %copy.15 = f32[4,8,4096]{2,1,0:T(8,128)} copy(f32[4,8,4096]{2,1,0:T(8,128)S(1)} %get-tuple-element.2) | data formatting | bytes 1048576
  53.2 0.7 %copy.16 = f32[4,2,4096]{2,1,0:T(2,128)} copy(f32[4,2,4096]{2,1,0:T(2,128)S(1)} %get-tuple-element.3) | data formatting | bytes 262144

commit v3 on v2

--- a/solution.py
+++ b/solution.py
@@ -434,18 +434,18 @@
     lax.fori_loop(0, 2, parts_coarse, 0)
     mask_coarse()
 
+    def fine(s, _):
+        factors_fine(s)
+        return 0
+
+    def coarse(s, _):
+        factors_coarse(s)
+        return 0
+
     @pl.when(fld == 0)
     def _():
-        def fine(s, _):
-            factors_fine(s)
-            return 0
-
-        def coarse(s, _):
-            factors_coarse(s)
-            return 0
-
-        lax.fori_loop(0, 4, fine, 0)
-        lax.fori_loop(0, 2, coarse, 0)
+        lax.fori_loop(0, 2, fine, 0)
+        lax.fori_loop(0, 1, coarse, 0)
 
     small[9].wait()
     wait_octants(0)
@@ -463,6 +463,11 @@
         return 0
 
     lax.fori_loop(0, FIELDS + 1, start, 0)
+
+    @pl.when(fld == 0)
+    def _():
+        lax.fori_loop(2, 4, fine, 0)
+        lax.fori_loop(1, 2, coarse, 0)
 
     def turn(t, _):
         late = jnp.where(t >= 5, 1, 0)

time: 54 us -> 52 us (0.963)
  Pallas kernels: 51.8 us -> 49.8 us
    pallas_call x1, Pallas kernels: 51.8 us -> 49.8 us  [shards(): pl.pallas_call(functools.partial(kernel, n), out_shape=(pltpu.VMEM(seed_f...]
where the time goes in v3:
time: 52 us; the launch traced here: 51.9 us
  Pallas kernels  49.8 us (96%)
  local copies, waits for them, and re-layouts  1.45 us (3%)
  between operations  0.64 us (1%)
    pallas_call x1, Pallas kernels, shards(): pl.pallas_call(functools.partial(kernel, n), out_shape=(pltpu.VMEM(seed_f...  49.8 us
    unnamed x2, local copies, waits for them, and re-layouts  1.45 us

profile of v3, /device:TPU:1, one launch (start us, length us, event | category | flops | bytes accessed | tf_op | source)
XLA Modules:
  0.0 51.9 jit_solution(12830529601306157386)
XLA Ops:
  0.6 49.8 %shard_map.122 = (f32[4,8,4096]{2,1,0:T(8,128)S(1)}, f32[4,2,4096]{2,1,0:T(2,128)S(1)}) custom-call(f32[4,8,4096]{2,1,0:T(8,128)} %seed_fine_in.1, f32[4,2,4096]{2,1,0:T(2,128)} %seed_coarse_in.1, f32[4,4,8,4096]{3,2,1,0:T(8,128)} %saved_fine_in.1, f32[2,4,2,4096]{3,2,1,0:T(2,128)} %saved_coarse_in.1, f32[4]{0:T(128)} %diffusion_in.1, f32[4]{0:T(128)} %shares_in.1, ...), custom_call_target="tpu_custom_call" | custom-call | tf_op jit(solution)/shard_map/pallas_call | solution.py:555
  50.4 0.8 %copy.15 = f32[4,8,4096]{2,1,0:T(8,128)} copy(f32[4,8,4096]{2,1,0:T(8,128)S(1)} %get-tuple-element.2) | data formatting | bytes 1048576
  51.2 0.7 %copy.16 = f32[4,2,4096]{2,1,0:T(2,128)} copy(f32[4,2,4096]{2,1,0:T(2,128)S(1)} %get-tuple-element.3) | data formatting | bytes 262144
